TPU v7x, 32 devices: a whole 2x2x4 slice. The times are simulated.
32 devices in a mesh: expert: 8 (over z, y), dp: 4 (over x, core).
Axes of the slice: x: 2, y: 2, z: 4, core: 2. Of those that a mesh axis runs over, the one named last changes fastest.
Arguments:
- tokens: bfloat16 [2048, 2880], P(('expert', 'dp')), may hold values from -6 to 6
- expert_ids: int32 [2048, 4], P(('expert', 'dp')), may hold values from 0 to 7, all different within a row; in each aligned block of 64 rows (0 to 63, 64 to 127, ...) at most 48 rows name the same one
- gate_logits: float32 [2048, 4], P(('expert', 'dp')), may hold values from -3 to 3
- w_gate: bfloat16 [8, 2880, 1536], P('expert', None, 'dp'), may hold values from -0.109375 to 0.109375
- w_up: bfloat16 [8, 2880, 1536], P('expert', None, 'dp'), may hold values from -0.109375 to 0.109375
- w_down: bfloat16 [8, 1536, 2880], P('expert', 'dp'), may hold values from -0.15625 to 0.15625
Outputs:
- mixed: bfloat16 [2048, 2880], P(('expert', 'dp'))
Inputs may be any that keep to these rules, and one draw needn't show every extreme that they name: `expert_ids`: each row names 4 different experts. Among the 64 rows of one device no expert is named more than 48 times, and every expert is named somewhere.
All inputs are finite; a program needn't handle non-finite values.
Results may differ from a plain program's by a relative error of at most 0.012.
Values may be sent and summed in bfloat16 or wider, within the bound.
A program may use at most 128 MiB of HBM per device.

v0:
```python
import jax
import jax.numpy as jnp
from jax import lax
from jax.sharding import PartitionSpec as P


def expert_rows(tile_in, gate_w, up_w, down_w):
    gate_val = jnp.dot(tile_in, gate_w, preferred_element_type=jnp.float32)
    up_val = jnp.dot(tile_in, up_w, preferred_element_type=jnp.float32)
    hidden = ((up_val + 1.0) * gate_val * jax.nn.sigmoid(1.702 * gate_val)).astype(jnp.bfloat16)
    return jnp.dot(hidden, down_w, preferred_element_type=jnp.float32).astype(jnp.bfloat16)


def run_tiles(packed, first_row, last_row, gate_w, up_w, down_w):
    tile_rows = 128
    n_tiles = jnp.maximum(last_row - first_row + tile_rows - 1, 0) // tile_rows
    result_buf = jnp.zeros((packed.shape[0], down_w.shape[1]), jnp.bfloat16)

    def advance(index_t, buffer):
        at_row = first_row + index_t * tile_rows
        tile_in = lax.dynamic_slice_in_dim(packed, at_row, tile_rows, 0)
        return lax.dynamic_update_slice_in_dim(
            buffer, expert_rows(tile_in, gate_w, up_w, down_w), at_row, 0
        )

    return lax.fori_loop(0, n_tiles, advance, result_buf)


def per_device(tokens, expert_ids, gate_logits, w_gate, w_up, w_down):
    n_rows, width = tokens.shape
    n_tops = expert_ids.shape[1]
    n_exp = lax.axis_size("expert")
    n_dp = lax.axis_size("dp")
    slot_cap = max(2, 3 * n_rows * n_tops // (2 * n_exp))
    tile_rows = 128
    flat_ids = expert_ids.reshape(-1)
    onehot = (flat_ids[:, None] == jnp.arange(n_exp, dtype=jnp.int32)[None, :]).astype(jnp.int32)
    rank_in = jnp.sum((jnp.cumsum(onehot, axis=0) - onehot) * onehot, axis=1)
    counts = jnp.sum(onehot, axis=0)
    slot_idx = flat_ids * slot_cap + rank_in
    source = (
        jnp.zeros((n_exp * slot_cap,), jnp.int32)
        .at[slot_idx]
        .set(jnp.arange(n_rows * n_tops, dtype=jnp.int32) // n_tops)
    )
    filled = (jnp.arange(slot_cap)[None, :] < counts[:, None]).reshape(-1)
    outgoing = jnp.where(filled[:, None], tokens[source], jnp.zeros_like(tokens[source])).reshape(
        n_exp, slot_cap, width
    )
    rows_mid, counts_mid = (
        lax.all_to_all(outgoing, "expert", split_axis=0, concat_axis=0, tiled=True),
        lax.all_to_all(counts[:, None], "expert", split_axis=0, concat_axis=0, tiled=True),
    )
    rows_in, counts_in = (
        lax.all_gather(rows_mid, "dp", axis=0, tiled=True),
        lax.all_gather(counts_mid, "dp", axis=0, tiled=True),
    )
    rows_flat = rows_in.reshape(-1, width)
    total_rows = rows_flat.shape[0]
    live_row = (jnp.arange(slot_cap)[None, :] < counts_in.reshape(-1)[:, None]).reshape(-1)
    position = jnp.cumsum(live_row.astype(jnp.int32)) - 1
    live_total = jnp.sum(live_row.astype(jnp.int32))
    padded = (total_rows + tile_rows - 1) // tile_rows * tile_rows + tile_rows
    gather_idx = (
        jnp.zeros((padded,), jnp.int32)
        .at[jnp.where(live_row, position, padded)]
        .set(jnp.arange(total_rows, dtype=jnp.int32), mode="drop")
    )
    packed = rows_flat[gather_idx]
    gate_w = w_gate[0]
    up_w = w_up[0]
    down_w = w_down[0]
    merged = run_tiles(packed, 0, live_total, gate_w, up_w, down_w)
    slot_out = jnp.where(
        live_row[:, None],
        merged[jnp.where(live_row, position, 0)],
        jnp.zeros((total_rows, width), jnp.bfloat16),
    )
    summed = lax.psum_scatter(
        slot_out.reshape(n_dp * n_exp, slot_cap, width), "dp", scatter_dimension=0, tiled=True
    ).astype(jnp.float32)
    expert_out = lax.all_to_all(
        summed.astype(jnp.bfloat16), "expert", split_axis=0, concat_axis=0, tiled=True
    )
    picked = expert_out.reshape(n_exp * slot_cap, width)[slot_idx]
    gate_wts = jnp.exp(gate_logits)
    gate_wts = gate_wts / jnp.sum(gate_wts, axis=1, keepdims=True)
    mixed = jnp.sum(
        picked.reshape(n_rows, n_tops, width).astype(jnp.float32) * gate_wts[:, :, None], axis=1
    )
    return mixed.astype(jnp.bfloat16)


def solution(mesh):
    return jax.shard_map(
        per_device,
        mesh=mesh,
        in_specs=(
            P(("expert", "dp"), None),
            P(("expert", "dp"), None),
            P(("expert", "dp"), None),
            P("expert", None, "dp"),
            P("expert", None, "dp"),
            P("expert", "dp", None),
        ),
        out_specs=P(("expert", "dp"), None),
        check_vma=False,
    )
```

profile of v0, /device:TPU:0, one launch (start us, length us, event | category | flops | bytes accessed | tf_op | source)
XLA Modules:
  0.0 431.5 jit_solution(1532442912530540609)
XLA Ops:
  6.5 0.0 copy-start
  6.5 0.0 all-gather.3.cloned.1.call-start
  6.5 0.8 copy.23
  7.4 0.1 eq.29
  7.5 0.1 eq.25
  7.6 0.7 broadcast_multiply_fusion
  8.3 0.6 reduce-window.15
  8.9 0.2 slice_reduce_fusion.1
  9.1 0.1 copy.25
  9.2 0.1 mul.41
  9.3 0.1 fusion.21
  9.5 1.4 scatter_custom_fusion
  10.9 0.1 iota_compare_fusion.3
  11.0 0.0 copy-done
  11.0 2.9 gather_fusion
  13.9 0.3 broadcast_select_fusion.1
  14.2 59.2 %all_to_all.22 = bf16[8,48,2880]{2,1,0:T(8,128)(2,1)} all-to-all(bf16[8,48,2880]{2,1,0:T(8,128)(2,1)S(1)} %broadcast_select_fusion.1), channel_id=1, replica_groups=mesh['expert'=8,'dp'=4] {'expert'}, dimensions={0} | all-to-all | bytes 4423680 | tf_op jit(solution)/shard_map/all_to_all | solution.py:51
  73.3 0.0 all-gather.3.cloned.1.call-update
  73.3 0.7 copy.24
  74.0 3.4 all-to-all-start
  77.4 0.0 reduce-scatter.2.cloned.1.call-start
  77.5 3.1 copy.27
  80.6 0.0 copy-done.3
  80.6 0.6 dynamic-slice
  81.8 2.1 all-to-all-done
  83.8 0.2 reduce.1
  84.1 0.2 dynamic-update-slice
  84.3 5.1 %all-reduce = s32[32]{0:T(128)S(1)} all-reduce(s32[32]{0:T(128)S(1)} %dynamic-update-slice), channel_id=2, replica_groups=mesh['expert'=8,'dp'=4] {'dp'}, use_global_device_ids=true, to_apply=%add | all-reduce | flops 32 | bytes 256
  89.4 0.7 convert_reduce_fusion.1
  90.8 0.1 fusion.29
  90.9 0.1 reshape.198
  91.0 0.3 reduce-window.19
  91.2 0.1 slice.26
  91.3 0.1 lt.106
  91.5 0.1 slice_reduce_fusion
  91.6 0.1 add_bitcast_fusion
  91.7 6.2 %scatter_custom_fusion.1 = s32[1664]{0:T(1024)S(1)} fusion(s32[1536]{0:T(1024)S(1)} %get-tuple-element.45, s32[1536]{0:T(1024)S(1)} %iota.22, s32[]{:T(128)} %constant.65.clone.1), kind=kCustom, calls=%fused_computation.54 | custom fusion | bytes 6660 | tf_op jit(solution)/shard_map/scatter | solution.py:67
  98.0 36.4 %all-gather.3.cloned.1.call-done = bf16[32,48,2880]{2,1,0:T(8,128)(2,1)} async-done(((bf16[8,48,2880]{2,1,0:T(8,128)(2,1)}), bf16[32,48,2880]{2,1,0:T(8,128)(2,1)}) %all-gather.3.cloned.1.call-update) | async-done | bytes 8847376 | tf_op jit(solution)/shard_map/all_gather | solution.py:55
  134.4 24.0 %gather_fusion.1 = bf16[1664,2880]{1,0:T(8,128)(2,1)} fusion(bf16[1536,2880]{1,0:T(8,128)(2,1)} %bitcast.35, s32[2048]{0:T(1024)S(1)} %pad_clamp_fusion.1), kind=kCustom, calls=%fused_computation.1 | custom fusion | bytes 19175936 | tf_op jit(solution)/shard_map/gather | solution.py:69
  158.4 4.3 %broadcast_in_dim.48 = bf16[1664,2880]{0,1:T(8,128)(2,1)} broadcast(bf16[]{:T(256)} %constant.66.clone.1), dimensions={} | broadcast | bytes 9584642 | tf_op jit(solution)/shard_map/broadcast_in_dim | solution.py:17
  162.7 32.8 %while.10 = (s32[]{:T(128)}, bf16[1664,2880]{0,1:T(8,128)(2,1)}, s32[]{:T(128)}, bf16[1664,2880]{1,0:T(8,128)(2,1)}, bf16[2880,384]{1,0:T(8,128)(2,1)}, /*index=...) while((s32[]{:T(128)}, bf16[1664,2880]{0,1:T(8,128)(2,1)}, ...), condition=%wide.region_10.11_spmd, body=%wide.region_9.10_spmd.sunk | while | flops 850108416 | bytes 9274527 | solution.py:26
  162.7 2.4 fusion.45
  165.1 4.1 fusion.46
  169.2 2.4 fusion.45
  171.7 4.2 fusion.46
  175.8 2.4 fusion.45
  178.2 4.1 fusion.46
  182.4 2.4 fusion.45
  184.8 4.2 fusion.46
  188.9 2.4 fusion.45
  191.3 4.1 fusion.46
  195.5 14.0 %copy.28 = bf16[1664,2880]{1,0:T(8,128)(2,1)} copy(bf16[1664,2880]{0,1:T(8,128)(2,1)} %get-tuple-element.43) | data formatting | bytes 19169280 | tf_op jit(solution)/shard_map/while | solution.py:26
  209.5 22.0 %gather_fusion.2 = bf16[1536,2880]{1,0:T(8,128)(2,1)} fusion(bf16[1664,2880]{1,0:T(8,128)(2,1)} %copy.28, s32[2048]{0:T(1024)S(1)} %pad_clamp_fusion), kind=kCustom, calls=%fused_computation.2 | custom fusion | bytes 17700864 | tf_op jit(solution)/shard_map/gather | solution.py:76
  231.5 8.0 %broadcast_select_fusion = bf16[32,48,2880]{2,1,0:T(8,128)(2,1)} fusion(bf16[32,48,2880]{2,1,0:T(8,128)(2,1)} %bitcast.40, pred[32,48]{1,0:T(8,128)(4,1)S(1)} %get-tuple-element.63), kind=kLoop, calls=%fused_computation.26 | loop fusion | flops 4423680 | bytes 17696256 | tf_op jit(solution)/shard_map/jit(_where)/select_n | solution.py:74
  239.5 0.0 reduce-scatter.2.cloned.1.call-update
  239.5 0.0 copy-start.2
  239.5 119.7 %reduce-scatter.2.cloned.1.call-done = bf16[8,48,2880]{2,1,0:T(8,128)(2,1)} async-done(((bf16[32,48,2880]{2,1,0:T(8,128)(2,1)}), bf16[8,48,2880]{2,1,0:T(8,128)(2,1)}) %reduce-scatter.2.cloned.1.call-update) | async-done | bytes 2211856 | tf_op jit(solution)/shard_map/reduce_scatter | solution.py:79
  359.2 5.5 %all-to-all-start.2 = ((bf16[8,48,2880]{2,1,0:T(8,128)(2,1)}), bf16[8,48,2880]{2,1,0:T(8,128)(2,1)S(1)}, u32[]{:S(2)}, u32[]{:S(2)}) async-start(bf16[8,48,2880]{2,1,0:T(8,128)(2,1)} %reduce-scatter.2.cloned.1.call-done), calls=%async_computation.3 | async-start | bytes 4521984 | tf_op jit(solution)/shard_map/all_to_all | solution.py:82
  364.8 0.0 copy-done.2
  364.8 0.1 copy.29
  364.9 51.4 %all-to-all-done.2 = bf16[8,48,2880]{2,1,0:T(8,128)(2,1)S(1)} async-done(((bf16[8,48,2880]{2,1,0:T(8,128)(2,1)}), bf16[8,48,2880]{2,1,0:T(8,128)(2,1)S(1)}, u32[]{:S(2)}, u32[]{:S(2)}) %all-to-all-start.2) | async-done | bytes 2211872 | tf_op jit(solution)/shard_map/all_to_all | solution.py:82
  416.4 2.7 gather_fusion.3
  419.0 2.8 reshape.199
  421.8 2.8 multiply_reduce_fusion
  (20 shorter events, 0.2 us)
Async XLA Ops:
  6.5 4.4 %copy-start = (bf16[64,2880]{1,0:T(8,128)(2,1)S(1)}, bf16[64,2880]{1,0:T(8,128)(2,1)}, u32[]{:S(2)}) copy-start(bf16[64,2880]{1,0:T(8,128)(2,1)} %param.8) | copy-start | bytes 1105924
  6.5 127.8 %all-gather.3.cloned.1.call-start = ((), (), s32[]{:S(2)}) async-start(), calls=%async_computation.4 | async-start | bytes 11304960 | tf_op jit(solution)/shard_map/all_gather | solution.py:55
  73.3 7.3 %copy-start.3 = (u32[32]{0:T(128)S(1)}, u32[32]{0:T(128)}, u32[]{:S(2)}) copy-start(u32[32]{0:T(128)} %constant.84) | copy-start | bytes 388
  74.0 9.8 %all-to-all-start = ((s32[8,1,1]{2,1,0:T(1,128)}), s32[8,1,1]{2,1,0:T(1,128)S(1)}, u32[]{:S(2)}, u32[]{:S(2)}) async-start(s32[8,1,1]{2,1,0:T(1,128)} %copy.24), calls=%async_computation | async-start | bytes 8192 | tf_op jit(solution)/shard_map/all_to_all | solution.py:52
  77.4 281.8 %reduce-scatter.2.cloned.1.call-start = ((), (), s32[]{:S(2)}) async-start(), calls=%async_computation.5 | async-start | bytes 11304960 | tf_op jit(solution)/shard_map/reduce_scatter | solution.py:79
  239.5 125.3 %copy-start.2 = (f32[64,4]{0,1:T(4,128)S(1)}, f32[64,4]{0,1:T(4,128)}, u32[]{:S(2)}) copy-start(f32[64,4]{0,1:T(4,128)} %param.10) | copy-start | bytes 3076
  359.2 57.1 %all-to-all-start.2 = ((bf16[8,48,2880]{2,1,0:T(8,128)(2,1)}), bf16[8,48,2880]{2,1,0:T(8,128)(2,1)S(1)}, u32[]{:S(2)}, u32[]{:S(2)}) async-start(bf16[8,48,2880]{2,1,0:T(8,128)(2,1)} %reduce-scatter.2.cloned.1.call-done), calls=%async_computation.3 | async-start | bytes 4521984 | tf_op jit(solution)/shard_map/all_to_all | solution.py:82
  416.4 8.3 %copy-start.1 = (bf16[64,2880]{1,0:T(8,128)(2,1)S(1)}, bf16[64,2880]{1,0:T(8,128)(2,1)}, u32[]{:S(2)}) copy-start(bf16[64,2880]{1,0:T(8,128)(2,1)} %param.8) | copy-start | bytes 1105924
Sparse Core Ops, SparseCore 0:
  73.5 60.8 all-gather.2
  239.6 119.5 reduce-scatter.1
where the time goes:
time: 434 us; the launch traced here: 431 us
  waiting for transfers between devices  210 us (48%)
  local copies, waits for them, and re-layouts  86.8 us (20%)
  blocking collectives  64.3 us (15%)
  matrix products  32.8 us (8%)
  between operations  14.8 us (3%)
  other arithmetic  14.1 us (3%)
  starting transfers between devices  8.97 us (2%)
    reduce_scatter x1, waiting for transfers between devices, per_device(): lax.psum_scatter(slot_out.reshape(n_dp * n_exp, slot_cap, width), 'dp', s...  120 us
    all_to_all x1, blocking collectives, per_device(): lax.all_to_all(outgoing, 'expert', split_axis=0, concat_axis=0, tiled=True)  59.2 us
    all_to_all x1, waiting for transfers between devices, per_device(): lax.all_to_all(summed.astype(jnp.bfloat16), 'expert', split_axis=0, conca...  51.4 us
    all_gather x1, waiting for transfers between devices, per_device(): lax.all_gather(rows_mid, 'dp', axis=0, tiled=True)  36.4 us
    gather x1, local copies, waits for them, and re-layouts, per_device(): packed = rows_flat[gather_idx]  24 us
    gather x1, local copies, waits for them, and re-layouts, per_device(): merged[jnp.where(live_row, position, 0)]  22 us
    dot_general x5, matrix products, expert_rows(): jnp.dot(hidden, down_w, preferred_element_type=jnp.float32)  20.7 us
    while x1, local copies, waits for them, and re-layouts, run_tiles(): return lax.fori_loop(0, n_tiles, advance, result_buf)  14 us
  transfers between devices with their start and end apart: 4, of which 4 were waited for; matrix products, arithmetic and copies ran while one was open for 3% of the time, Pallas kernels for 0%

commit v1 on v0

--- a/solution.py
+++ b/solution.py
@@ -1,6 +1,10 @@
+import functools
+
 import jax
 import jax.numpy as jnp
 from jax import lax
+from jax.experimental import pallas as pl
+from jax.experimental.pallas import tpu as pltpu
 from jax.sharding import PartitionSpec as P
 
 
@@ -26,7 +30,7 @@
     return lax.fori_loop(0, n_tiles, advance, result_buf)
 
 
-def per_device(tokens, expert_ids, gate_logits, w_gate, w_up, w_down):
+def sparse_device(tokens, expert_ids, gate_logits, w_gate, w_up, w_down):
     n_rows, width = tokens.shape
     n_tops = expert_ids.shape[1]
     n_exp = lax.axis_size("expert")
@@ -91,7 +95,332 @@
     return mixed.astype(jnp.bfloat16)
 
 
+LANES = 128
+CHUNKS = 1
+
+
+def round_up(value, step):
+    return (value + step - 1) // step * step
+
+
+def routing_columns(expert_ids, gate_logits, n_exp, lanes):
+    gate_wts = jnp.exp(gate_logits)
+    gate_wts = gate_wts / jnp.sum(gate_wts, axis=1, keepdims=True)
+    chosen = expert_ids[:, :, None] == jnp.arange(n_exp, dtype=jnp.int32)[None, None, :]
+    by_expert = jnp.sum(jnp.where(chosen, gate_wts[:, :, None], 0.0), axis=1)
+    high = by_expert.astype(jnp.bfloat16)
+    low = (by_expert - high.astype(jnp.float32)).astype(jnp.bfloat16)
+    columns = jnp.concatenate([high, low], axis=1)
+    return jnp.pad(columns, ((0, 0), (0, lanes - columns.shape[1])))
+
+
+def dense_kernel(n_exp, rows_ref, gate_ref, up_ref, down_ref, out_ref):
+    width, hidden_width = gate_ref.shape
+    lanes = rows_ref.shape[1]
+    mine = lax.axis_index("expert")
+    rows_in = rows_ref[:, :width]
+    gate_val = jnp.dot(rows_in, gate_ref[...], preferred_element_type=jnp.float32)
+    up_val = jnp.dot(rows_in, up_ref[...], preferred_element_type=jnp.float32)
+    first = width // LANES * LANES
+    extra = rows_ref[:, first:lanes].astype(jnp.float32)
+    lane = lax.broadcasted_iota(jnp.int32, extra.shape, 1) + first - width
+    weight = jnp.sum(jnp.where((lane == mine) | (lane == mine + n_exp), extra, 0.0), axis=1, keepdims=True)
+    hidden = (up_val + 1.0) * gate_val * (weight / (1.0 + jnp.exp(-1.702 * gate_val)))
+    out_ref[...] = jnp.dot(
+        hidden.astype(jnp.bfloat16), down_ref[...], preferred_element_type=jnp.float32
+    ).astype(out_ref.dtype)
+
+
+def dense_rows(rows, gate_w, up_w, down_w, n_exp):
+    n_rows, lanes = rows.shape
+    width, hidden_width = gate_w.shape
+    tile_rows = 256
+    while n_rows % tile_rows:
+        tile_rows //= 2
+    whole = pl.BlockSpec(memory_space=pltpu.VMEM)
+    return pl.pallas_call(
+        functools.partial(dense_kernel, n_exp),
+        grid=(n_rows // tile_rows,),
+        in_specs=[pl.BlockSpec((tile_rows, lanes), lambda i: (i, 0)), whole, whole, whole],
+        out_specs=pl.BlockSpec((tile_rows, width), lambda i: (i, 0)),
+        out_shape=jax.ShapeDtypeStruct((n_rows, width), jnp.bfloat16),
+        cost_estimate=pl.CostEstimate(
+            flops=6 * n_rows * width * hidden_width,
+            bytes_accessed=2 * n_rows * (lanes + width) + 6 * width * hidden_width,
+            transcendentals=n_rows * hidden_width,
+        ),
+    )(rows, gate_w, up_w, down_w)
+
+
+def dense_device(tokens, expert_ids, gate_logits, w_gate, w_up, w_down):
+    n_rows, width = tokens.shape
+    n_exp = lax.axis_size("expert")
+    both = ("expert", "dp")
+    lanes = round_up(width + 2 * n_exp, LANES)
+    extra = routing_columns(expert_ids, gate_logits, n_exp, lanes - width)
+    wide = jnp.concatenate([tokens, extra], axis=1)
+    step = n_rows // CHUNKS
+    done = []
+    for chunk in range(CHUNKS):
+        rows = lax.all_gather(wide[chunk * step : (chunk + 1) * step], both, axis=0, tiled=True)
+        partial = dense_rows(rows, w_gate[0], w_up[0], w_down[0], n_exp)
+        done.append(lax.psum_scatter(partial, both, scatter_dimension=0, tiled=True))
+    return done[0] if CHUNKS == 1 else jnp.concatenate(done, axis=0)
+
+
+def tile_product(n_exp, rows_in, extra, gate_ref, up_ref, down_ref):
+    width = gate_ref.shape[0]
+    mine = lax.axis_index("expert")
+    gate_val = jnp.dot(rows_in, gate_ref[...], preferred_element_type=jnp.float32)
+    up_val = jnp.dot(rows_in, up_ref[...], preferred_element_type=jnp.float32)
+    extra = extra.astype(jnp.float32)
+    lane = lax.broadcasted_iota(jnp.int32, extra.shape, 1) - width % LANES
+    weight = jnp.sum(jnp.where((lane == mine) | (lane == mine + n_exp), extra, 0.0), axis=1, keepdims=True)
+    hidden = (up_val + 1.0) * gate_val * (weight / (1.0 + jnp.exp(-1.702 * gate_val)))
+    return jnp.dot(hidden.astype(jnp.bfloat16), down_ref[...], preferred_element_type=jnp.float32)
+
+
+def fused_kernel(
+    n_exp, wide_ref, gate_hbm, up_hbm, down_hbm, out_ref,
+    held, part, core_in, x_in, y_in, x_diag, y_diag, z_in,
+    gate_ref, up_ref, down_ref, send_sem, recv_sem, load_sem,
+):
+    n_z = n_exp // 2
+    n_rows, width = out_ref.shape
+    lanes = wide_ref.shape[1]
+    half = n_rows // 2
+    spare = width // LANES * LANES
+    expert, dp = lax.axis_index("expert"), lax.axis_index("dp")
+    z, y = lax.div(expert, 2), lax.rem(expert, 2)
+    x, core = lax.div(dp, 2), lax.rem(dp, 2)
+    to_x = (expert, (1 - x) * 2 + core)
+    to_y = (z * 2 + 1 - y, dp)
+    to_core = (expert, x * 2 + 1 - core)
+
+    def at_z(d):
+        return lax.rem(z + d, n_z)
+
+    def to_z(d):
+        return (at_z(d) * 2 + y, dp)
+
+    columns = {"o": y * 2 + x, "x": y * 2 + 1 - x, "y": (1 - y) * 2 + x, "d": (1 - y) * 2 + 1 - x}
+
+    def block(column, which, zz=0):
+        return (columns[column] * 2 + which) * n_z + zz
+
+    copies = {}
+
+    def start(key, source, target, device):
+        number = len(copies)
+        copies[key] = pltpu.make_async_remote_copy(
+            src_ref=source,
+            dst_ref=target,
+            send_sem=send_sem.at[number],
+            recv_sem=recv_sem.at[number],
+            device_id=device,
+            device_id_type=pl.DeviceIdType.MESH,
+        )
+        copies[key].start()
+
+    def arrived(*key):
+        copies[key].wait_recv()
+
+    loads = [
+        pltpu.make_async_copy(source, target, load_sem.at[i])
+        for i, (source, target) in enumerate(((gate_hbm, gate_ref), (up_hbm, up_ref), (down_hbm, down_ref)))
+    ]
+    for load in loads:
+        load.start()
+
+    partners = [to_x, to_y, to_core] + [to_z(d) for d in range(1, n_z)]
+    barrier = pltpu.get_barrier_semaphore()
+    for partner in partners:
+        pl.semaphore_signal(barrier, inc=1, device_id=partner, device_id_type=pl.DeviceIdType.MESH)
+    pl.semaphore_wait(barrier, len(partners))
+
+    near = sorted(range(1, n_z), key=lambda d: min(d, n_z - d))
+    own = held.at[block("o", core, z)]
+    start(("x", 0), wide_ref, own, to_x)
+    start(("y", 0), wide_ref, own, to_y)
+    for d in near:
+        start(("z", d), wide_ref, own, to_z(d))
+    start(("co", 0), wide_ref, own, to_core)
+    own[...] = wide_ref[...]
+
+    def relay_z(d):
+        arrived("z", d)
+        source = held.at[block("o", core, at_z(n_z - d))]
+        start(("x", d), source, source, to_x)
+        start(("y", d), source, source, to_y)
+        start(("co", d), source, source, to_core)
+
+    def relay_xy(d):
+        zz = at_z(n_z - d)
+        arrived("x", d)
+        source = held.at[block("x", core, zz)]
+        upper = held.at[block("x", core, zz), pl.ds(0, half)]
+        start(("y2", d), upper, upper, to_y)
+        start(("cx", d), source, source, to_core)
+        arrived("y", d)
+        source = held.at[block("y", core, zz)]
+        lower = held.at[block("y", core, zz), pl.ds(half, half)]
+        start(("x2", d), lower, lower, to_x)
+        start(("cy", d), source, source, to_core)
+
+    def relay_diag(d):
+        source = held.at[block("d", core, at_z(n_z - d))]
+        arrived("x2", d)
+        arrived("y2", d)
+        start(("cd", d), source, source, to_core)
+
+    def product(column, which):
+        span = pl.ds(block(column, which), n_z)
+        rows_in = held[span, :, :width].reshape(n_z * n_rows, width)
+        extra = held[span, :, spare:lanes].reshape(n_z * n_rows, lanes - spare)
+        result = tile_product(n_exp, rows_in, extra, gate_ref, up_ref, down_ref)
+        part[span] = result.astype(part.dtype).reshape(n_z, n_rows, width)
+
+    order = "oxyd"
+
+    def swap(column):
+        for d in range(n_z):
+            arrived("c" + column, d)
+        product(column, 1 - core)
+        start(("p", column), part.at[pl.ds(block(column, 1 - core), n_z)], core_in.at[order.index(column)], to_core)
+
+    def combine(column):
+        arrived("p", column)
+        place = order.index(column)
+        base = block(column, core)
+
+        @pl.loop(0, n_z)
+        def _(zz):
+            part[base + zz] = part[base + zz] + core_in[place, zz]
+
+    waiting = [0]
+    for d in near:
+        relay_z(d)
+        if d == near[-1]:
+            for load in loads:
+                load.wait()
+            product("o", core)
+        relay_xy(waiting.pop())
+        waiting.append(d)
+    swap("o")
+    relay_xy(waiting.pop())
+    product("x", core)
+    swap("x")
+    relay_diag(0)
+    product("y", core)
+    for d in near[:-1]:
+        relay_diag(d)
+    swap("y")
+    relay_diag(near[-1])
+    combine("x")
+    rows_x = pl.ds(block("x", core), n_z)
+    start(("ex",), part.at[rows_x, pl.ds(half, half)], x_in.at[:, pl.ds(half, half)], to_x)
+    combine("y")
+    rows_y = pl.ds(block("y", core), n_z)
+    start(("ey",), part.at[rows_y, pl.ds(0, half)], y_in.at[:, pl.ds(0, half)], to_y)
+    product("d", core)
+    swap("d")
+    combine("d")
+    far = near[::-1] + [0]
+    for d in far:
+        source = block("d", core, at_z(d))
+        start(("dx", d), part.at[source, pl.ds(half, half)], x_diag.at[d], to_x)
+        start(("dy", d), part.at[source, pl.ds(0, half)], y_diag.at[d], to_y)
+    combine("o")
+
+    def gather_diag(d):
+        zz = at_z(d)
+        arrived("dx", d)
+        spot = block("y", core, zz)
+        part[spot, half:] = part[spot, half:] + x_diag[d]
+        start(("fy", d), part.at[spot, pl.ds(half, half)], y_in.at[zz, pl.ds(half, half)], to_y)
+        arrived("dy", d)
+        spot = block("x", core, zz)
+        part[spot, :half] = part[spot, :half] + y_diag[d]
+        start(("fx", d), part.at[spot, pl.ds(0, half)], x_in.at[zz, pl.ds(0, half)], to_x)
+
+    def gather_xy(d):
+        zz = at_z(d)
+        arrived("fx", d)
+        arrived("fy", d)
+        total = (
+            part[block("o", core, zz)].astype(jnp.float32)
+            + x_in[zz].astype(jnp.float32)
+            + y_in[zz].astype(jnp.float32)
+        )
+        if d == 0:
+            for other in far[:-1]:
+                arrived("s", other)
+                total = total + z_in[other - 1].astype(jnp.float32)
+            out_ref[...] = total.astype(out_ref.dtype)
+        else:
+            spot = block("o", core, zz)
+            part[spot] = total.astype(part.dtype)
+            start(("s", d), part.at[spot], z_in.at[d - 1], to_z(d))
+
+    gather_diag(far[0])
+    arrived("ex")
+    arrived("ey")
+    for before, d in zip(far, far[1:]):
+        gather_diag(d)
+        gather_xy(before)
+    gather_xy(far[-1])
+    for copy in copies.values():
+        copy.wait_send()
+
+
+def fused_device(tokens, expert_ids, gate_logits, w_gate, w_up, w_down):
+    n_rows, width = tokens.shape
+    hidden_width = w_gate.shape[2]
+    n_exp = lax.axis_size("expert")
+    n_z = n_exp // 2
+    lanes = round_up(width + 2 * n_exp, LANES)
+    extra = routing_columns(expert_ids, gate_logits, n_exp, lanes - width)
+    wide = jnp.concatenate([tokens, extra], axis=1)
+    total = n_exp * lax.axis_size("dp")
+    messages = 8 * n_z + 4 * n_z + 4 + 2 + 4 * n_z + n_z + n_z
+    bf16 = jnp.bfloat16
+    in_vmem = pl.BlockSpec(memory_space=pltpu.VMEM)
+    anywhere = pl.BlockSpec(memory_space=pl.ANY)
+    return pl.pallas_call(
+        functools.partial(fused_kernel, n_exp),
+        in_specs=[in_vmem, anywhere, anywhere, anywhere],
+        out_specs=in_vmem,
+        out_shape=jax.ShapeDtypeStruct((n_rows, width), bf16),
+        scratch_shapes=[
+            pltpu.VMEM((total, n_rows, lanes), bf16),
+            pltpu.VMEM((total, n_rows, width), bf16),
+            pltpu.VMEM((4, n_z, n_rows, width), bf16),
+            pltpu.VMEM((n_z, n_rows, width), bf16),
+            pltpu.VMEM((n_z, n_rows, width), bf16),
+            pltpu.VMEM((n_z, n_rows // 2, width), bf16),
+            pltpu.VMEM((n_z, n_rows // 2, width), bf16),
+            pltpu.VMEM((n_z - 1, n_rows, width), bf16),
+            pltpu.VMEM((width, hidden_width), bf16),
+            pltpu.VMEM((width, hidden_width), bf16),
+            pltpu.VMEM((hidden_width, width), bf16),
+            pltpu.SemaphoreType.DMA((messages,)),
+            pltpu.SemaphoreType.DMA((messages,)),
+            pltpu.SemaphoreType.DMA((3,)),
+        ],
+        compiler_params=pltpu.CompilerParams(
+            collective_id=0, has_side_effects=True, vmem_limit_bytes=64 * 1024 * 1024 - 65536
+        ),
+    )(wide, w_gate[0], w_up[0], w_down[0])
+
+
 def solution(mesh):
+    def per_device(tokens, expert_ids, *others):
+        n_exp = lax.axis_size("expert")
+        if n_exp > 4 * expert_ids.shape[1]:
+            return sparse_device(tokens, expert_ids, *others)
+        paired = lax.axis_size("dp") == 4 and n_exp % 2 == 0 and tokens.shape[0] % 32 == 0
+        return (fused_device if paired else dense_device)(tokens, expert_ids, *others)
+
     return jax.shard_map(
         per_device,
         mesh=mesh,

time: 434 us -> 149 us (0.34)
  waiting for transfers between devices: 210 us -> 0 us
  Pallas kernels: 0 us -> 136 us
  local copies, waits for them, and re-layouts: 86.8 us -> 6.04 us
  blocking collectives: 64.3 us -> 0 us
  matrix products: 32.8 us -> 0 us
  between operations: 14.8 us -> 0.02 us
  other arithmetic: 14.1 us -> 3.91 us
  starting transfers between devices: 8.97 us -> 0 us
    pallas_call x0 -> x1, Pallas kernels: none -> 136 us  [fused_device(): pl.pallas_call(functools.partial(fused_kernel, n_exp), in_specs=[in_vmem,...]
    reduce_scatter x1 -> x0, waiting for transfers between devices: 120 us -> none  [per_device(): lax.psum_scatter(slot_out.reshape(n_dp * n_exp, slot_cap, width), 'dp', s...]
    all_to_all x1 -> x0, blocking collectives: 59.2 us -> none  [per_device(): lax.all_to_all(outgoing, 'expert', split_axis=0, concat_axis=0, tiled=True)]
    all_to_all x2 -> x0, waiting for transfers between devices: 53.5 us -> none  [the longest x1 51.4 us: per_device(): lax.all_to_all(summed.astype(jnp.bfloat16), 'expert', split_axis=0, conca...]
    gather x4 -> x0, local copies, waits for them, and re-layouts: 51.5 us -> none  [the longest x1 24 us: per_device(): packed = rows_flat[gather_idx]]
    all_gather x1 -> x0, waiting for transfers between devices: 36.4 us -> none  [per_device(): lax.all_gather(rows_mid, 'dp', axis=0, tiled=True)]
    dot_general x10 -> x0, matrix products: 32.8 us -> none  [the longest x5 20.7 us: expert_rows(): jnp.dot(hidden, down_w, preferred_element_type=jnp.float32)]
    while x1 -> x0, local copies, waits for them, and re-layouts: 14 us -> none  [run_tiles(): return lax.fori_loop(0, n_tiles, advance, result_buf)]
  transfers between devices with their start and end apart: 4 -> 0, of which waited for: 4 -> 0; matrix products, arithmetic and copies ran while one was open for 3% -> 0% of each run, Pallas kernels for 0% -> 0%
where the time goes in v1:
time: 149 us; the launch traced here: 146 us
  Pallas kernels  136 us (91%)
  local copies, waits for them, and re-layouts  6.04 us (4%)
  other arithmetic  3.91 us (3%)
    pallas_call x1, Pallas kernels, fused_device(): pl.pallas_call(functools.partial(fused_kernel, n_exp), in_specs=[in_vmem,...  136 us
    unnamed x2, local copies, waits for them, and re-layouts  5.94 us

profile of v1, /device:TPU:0, one launch (start us, length us, event | category | flops | bytes accessed | tf_op | source)
XLA Modules:
  0.0 145.8 jit_solution(9124215876773489585)
XLA Ops:
  0.0 0.7 exponential_reduce_fusion
  0.7 0.7 exponential_divide_fusion
  1.4 0.7 select_reduce_fusion
  2.1 0.1 copy.14
  2.2 1.8 %fusion.1.wide_ref = bf16[64,2944]{1,0:T(8,128)(2,1)} fusion(bf16[64,16]{1,0:T(8,128)(2,1)S(1)} %copy.14, bf16[64,2880]{1,0:T(8,128)(2,1)} %param.6), kind=kLoop, calls=%fused_computation.2 | loop fusion | flops 1130496 | bytes 747520 | tf_op jit(solution)/shard_map/concatenate | solution.py:383
  4.0 4.2 %copy.15 = bf16[1,384,2880]{2,1,0:T(8,128)(2,1)} copy(bf16[1,384,2880]{1,2,0:T(8,128)(2,1)} %param.11) | data formatting | bytes 4423680 | tf_op args[5]
  8.2 135.9 %shard_map.64 = bf16[64,2880]{1,0:T(8,128)(2,1)} custom-call(bf16[64,2944]{1,0:T(8,128)(2,1)} %fusion.1.wide_ref, bf16[2880,384]{1,0:T(8,128)(2,1)} %bitcast.4, bf16[2880,384]{1,0:T(8,128)(2,1)} %bitcast.5, bf16[384,2880]{1,0:T(8,128)(2,1)} %bitcast.3), custom_call_target="tpu_custom_call" | custom-call | tf_op jit(solution)/shard_map/pallas_call | solution.py:389
  144.1 1.8 %copy.17 = bf16[64,2880]{1,0:T(8,128)(2,1)} copy(bf16[64,2880]{1,0:T(8,128)(2,1)} %shard_map.64) | data formatting | bytes 737280
  (2 shorter events, 0.0 us)

commit v2 on v1

--- a/solution.py
+++ b/solution.py
@@ -177,7 +177,12 @@
     lane = lax.broadcasted_iota(jnp.int32, extra.shape, 1) - width % LANES
     weight = jnp.sum(jnp.where((lane == mine) | (lane == mine + n_exp), extra, 0.0), axis=1, keepdims=True)
     hidden = (up_val + 1.0) * gate_val * (weight / (1.0 + jnp.exp(-1.702 * gate_val)))
-    return jnp.dot(hidden.astype(jnp.bfloat16), down_ref[...], preferred_element_type=jnp.float32)
+    return lax.dot_general(
+        hidden.astype(jnp.bfloat16),
+        down_ref[...],
+        (((1,), (1,)), ((), ())),
+        preferred_element_type=jnp.float32,
+    )
 
 
 def fused_kernel(
@@ -314,15 +319,15 @@
     product("y", core)
     for d in near[:-1]:
         relay_diag(d)
-    swap("y")
-    relay_diag(near[-1])
     combine("x")
     rows_x = pl.ds(block("x", core), n_z)
     start(("ex",), part.at[rows_x, pl.ds(half, half)], x_in.at[:, pl.ds(half, half)], to_x)
+    swap("y")
+    relay_diag(near[-1])
+    product("d", core)
     combine("y")
     rows_y = pl.ds(block("y", core), n_z)
     start(("ey",), part.at[rows_y, pl.ds(0, half)], y_in.at[:, pl.ds(0, half)], to_y)
-    product("d", core)
     swap("d")
     combine("d")
     far = near[::-1] + [0]
@@ -402,7 +407,7 @@
             pltpu.VMEM((n_z - 1, n_rows, width), bf16),
             pltpu.VMEM((width, hidden_width), bf16),
             pltpu.VMEM((width, hidden_width), bf16),
-            pltpu.VMEM((hidden_width, width), bf16),
+            pltpu.VMEM((width, hidden_width), bf16),
             pltpu.SemaphoreType.DMA((messages,)),
             pltpu.SemaphoreType.DMA((messages,)),
             pltpu.SemaphoreType.DMA((3,)),
@@ -410,7 +415,7 @@
         compiler_params=pltpu.CompilerParams(
             collective_id=0, has_side_effects=True, vmem_limit_bytes=64 * 1024 * 1024 - 65536
         ),
-    )(wide, w_gate[0], w_up[0], w_down[0])
+    )(wide, w_gate[0], w_up[0], w_down[0].T)
 
 
 def solution(mesh):

time: 149 us -> 145 us (0.973)
  local copies, waits for them, and re-layouts: 6.04 us -> 1.86 us
    unnamed x2 -> x1, local copies, waits for them, and re-layouts: 5.94 us -> 1.76 us
    pallas_call x1, Pallas kernels: 136 us -> 137 us  [fused_device(): pl.pallas_call(functools.partial(fused_kernel, n_exp), in_specs=[in_vmem,...]
where the time goes in v2:
time: 145 us; the launch traced here: 143 us
  Pallas kernels  137 us (94%)
  other arithmetic  3.91 us (3%)
  local copies, waits for them, and re-layouts  1.86 us (1%)
    pallas_call x1, Pallas kernels, fused_device(): pl.pallas_call(functools.partial(fused_kernel, n_exp), in_specs=[in_vmem,...  137 us

profile of v2, /device:TPU:0, one launch (start us, length us, event | category | flops | bytes accessed | tf_op | source)
XLA Modules:
  0.0 143.2 jit_solution(16579298684022932414)
XLA Ops:
  0.0 0.7 exponential_reduce_fusion
  0.7 0.7 exponential_divide_fusion
  1.4 0.7 select_reduce_fusion
  2.1 0.1 copy.12
  2.2 1.8 %fusion.1.wide_ref = bf16[64,2944]{1,0:T(8,128)(2,1)} fusion(bf16[64,16]{1,0:T(8,128)(2,1)S(1)} %copy.12, bf16[64,2880]{1,0:T(8,128)(2,1)} %param.6), kind=kLoop, calls=%fused_computation.2 | loop fusion | flops 1130496 | bytes 747520 | tf_op jit(solution)/shard_map/concatenate | solution.py:388
  4.0 137.4 %shard_map.64 = bf16[64,2880]{1,0:T(8,128)(2,1)} custom-call(bf16[64,2944]{1,0:T(8,128)(2,1)} %fusion.1.wide_ref, bf16[2880,384]{1,0:T(8,128)(2,1)} %bitcast.5, bf16[2880,384]{1,0:T(8,128)(2,1)} %bitcast.6, bf16[2880,384]{1,0:T(8,128)(2,1)} %bitcast.7), custom_call_target="tpu_custom_call" | custom-call | tf_op jit(solution)/shard_map/pallas_call | solution.py:394
  141.4 1.8 %copy.14 = bf16[64,2880]{1,0:T(8,128)(2,1)} copy(bf16[64,2880]{1,0:T(8,128)(2,1)} %shard_map.64) | data formatting | bytes 737280
  (2 shorter events, 0.0 us)
